TPU v7x, 256 devices: a whole 4x4x8 slice. The times are simulated.
256 devices in a mesh: fsdp: 16 (over y, x), width: 16 (over z, core).
Axes of the slice: x: 4, y: 4, z: 8, core: 2. Of those that a mesh axis runs over, the one named last changes fastest.
Arguments:
- train_gate: float32 [4096, 11008], P('fsdp', 'width'), may hold values from -0.125 to 0.125
- drift_gate: float32 [4096, 11008], P('fsdp', 'width'), may hold values from -0.09375 to 0.09375
- spread_gate: float32 [4096, 11008], P('fsdp', 'width'), may hold values from -0.09375 to 0.09375
- train_up: float32 [4096, 11008], P('fsdp', 'width'), may hold values from -0.125 to 0.125
- drift_up: float32 [4096, 11008], P('fsdp', 'width'), may hold values from -0.09375 to 0.09375
- spread_up: float32 [4096, 11008], P('fsdp', 'width'), may hold values from -0.09375 to 0.09375
- norm_train: float32 [4096], P(('fsdp', 'width')), may hold values from 0.25 to 1.75
- norm_step: float32 [4096], P(('fsdp', 'width')), may hold values from -0.3 to 0.3
Outputs:
- serving_gate: bfloat16 [4096, 11008], P(None, 'width')
- serving_up: bfloat16 [4096, 11008], P(None, 'width')
- scale_gate: float32 [11008], P('width')
- scale_up: float32 [11008], P('width')
- serve_norm: bfloat16 [4096], replicated
- whole_gate: float32 [4096, 11008], P('fsdp', 'width')
- whole_up: float32 [4096, 11008], P('fsdp', 'width')
All inputs are finite; a program needn't handle non-finite values.
Results may differ from a plain program's by a relative error of at most 0.0004.
Values may be sent and summed in bfloat16 or wider, within the bound.
No kernel may reach another device: no remote copies, remote signals or barrier semaphores. Data moves between devices by JAX's collectives and lax.ppermute only.
A program may use at most 128 MiB of HBM per device.

v0:
```python
import jax
import jax.numpy as jnp
from jax import lax
from jax.sharding import Mesh
from jax.sharding import PartitionSpec as P

FSDP = ("fsdp_0", "fsdp_1")
FSDP_WIDTH = ("fsdp_0", "fsdp_1", "width")


learn_rate = 0.3
hold_rate = 0.9


def one_axis_at_a_time(array, axes):
    for axis in axes:
        array = lax.psum(array, axis)
    return array


def side_by_side(arrays, axis, dim, along):
    both = jnp.concatenate(arrays, axis=along)
    result, at, done = (lax.all_gather(both, axis, axis=dim, tiled=True), 0, [])
    for a in arrays:
        done.append(lax.slice_in_dim(result, at, at + a.shape[along], axis=along))
        at += a.shape[along]
    return tuple(done)


def shards(
    train_gate, drift_gate, spread_gate, train_up, drift_up, spread_up, norm_train, norm_step
):
    hold_gate = hold_rate * drift_gate + spread_gate
    whole_gate = train_gate - learn_rate * hold_gate
    hold_up = hold_rate * drift_up + spread_up
    whole_up = train_up - learn_rate * hold_up
    total_gate, total_up = (
        one_axis_at_a_time(jnp.sum(whole_gate * whole_gate, axis=0), FSDP),
        one_axis_at_a_time(jnp.sum(whole_up * whole_up, axis=0), FSDP),
    )
    scale_gate = jnp.sqrt(total_gate)
    scale_up = jnp.sqrt(total_up)
    narrow_gate, narrow_up = (
        (whole_gate / scale_gate).astype(jnp.bfloat16),
        (whole_up / scale_up).astype(jnp.bfloat16),
    )
    serving_gate, serving_up = side_by_side((narrow_gate, narrow_up), FSDP, 0, 1)
    serve_norm = lax.all_gather(
        (norm_train + norm_step).astype(jnp.bfloat16), FSDP_WIDTH, axis=0, tiled=True
    )
    return (serving_gate, serving_up, scale_gate, scale_up, serve_norm, whole_gate, whole_up)


def solution(mesh):
    split = Mesh(mesh.devices.reshape(4, 4, mesh.shape["width"]), ("fsdp_0", "fsdp_1", "width"))
    in_specs = (
        P(FSDP, "width"),
        P(FSDP, "width"),
        P(FSDP, "width"),
        P(FSDP, "width"),
        P(FSDP, "width"),
        P(FSDP, "width"),
        P(FSDP_WIDTH),
        P(FSDP_WIDTH),
    )
    out_specs = (
        P(None, "width"),
        P(None, "width"),
        P("width"),
        P("width"),
        P(),
        P(FSDP, "width"),
        P(FSDP, "width"),
    )
    return jax.shard_map(
        shards, mesh=split, in_specs=in_specs, out_specs=out_specs, check_vma=False
    )
```

profile of v0, /device:TPU:2, one launch (start us, length us, event | category | flops | bytes accessed | tf_op | source)
XLA Modules:
  0.0 145.8 jit_solution(3862906683493786616)
XLA Ops:
  7.2 0.0 copy-start.4
  7.2 0.0 copy-start.5
  7.2 0.0 all-gather.2.cloned.1.call-start
  7.2 2.5 %multiply_reduce_fusion = (f32[688]{0:T(1024)S(1)}, f32[256,688]{0,1:T(8,128)S(1)}, f32[688]{0:T(1024)S(1)}, f32[256,688]{0,1:T(8,128)S(1)}) fusion(f32[256,688]{0,1:T(8,128)} %param.11, f32[256,688]{0,1:T(8,128)} %param.13, f32[256,688]{0,1:T(8,128)} %param.12, f32[256,688]{0,1:T(8,128)} %param.8, f32[256,688]{0,1:T(8,128)} %param.10, f32[256,688]{0,1:T(8,128)} %param.9), kind=kLoop, calls=%fused_computation.2 | loop fusion | flops 2112160 | bytes 5641600 | tf_op jit(solution)/shard_map/reduce_sum | solution.py:39
  9.8 0.0 copy-start
  9.8 0.0 copy-start.1
  9.8 10.9 %all-reduce.2 = (f32[688]{0:T(1024)S(1)}, f32[688]{0:T(1024)S(1)}) all-reduce(f32[688]{0:T(1024)S(1)} %get-tuple-element.13, f32[688]{0:T(1024)S(1)} %get-tuple-element.17), channel_id=1, replica_groups=mesh['fsdp_0'=4,'fsdp_1'=4,'width'=16] {'fsdp_0'}, use_global_device_ids=true, to_apply=%region_4.0 | all-reduce | flops 1376 | bytes 11008 | tf_op jit(solution)/shard_map/psum | solution.py:17
  20.7 8.8 %all-reduce.1 = (f32[688]{0:T(1024)S(1)}, f32[688]{0:T(1024)S(1)}) all-reduce(f32[688]{0:T(1024)S(1)} %get-tuple-element.9, f32[688]{0:T(1024)S(1)} %get-tuple-element.10), channel_id=1, replica_groups=mesh['fsdp_0'=4,'fsdp_1'=4,'width'=16] {'fsdp_1'}, use_global_device_ids=true, to_apply=%region_5.0 | all-reduce | flops 1376 | bytes 11008 | tf_op jit(solution)/shard_map/psum | solution.py:17
  29.5 0.0 copy-start.2
  29.5 0.0 copy-start.3
  29.5 0.2 divide_convert_fusion.1
  29.7 0.2 divide_convert_fusion
  29.9 0.9 pad_maximum_fusion
  30.8 0.0 all-gather.2.cloned.1.call-update
  30.8 0.0 copy-done.4
  30.8 0.0 copy-done.5
  30.8 0.2 dynamic-update-slice
  31.1 80.0 %all-reduce = bf16[4096]{0:T(1024)(128)(2,1)} all-reduce(bf16[4096]{0:T(1024)(128)(2,1)S(1)} %dynamic-update-slice), channel_id=1, replica_groups=mesh['fsdp_0'=4,'fsdp_1'=4,'width'=16] {'fsdp_0','fsdp_1','width'}, use_global_device_ids=true, to_apply=%add | all-reduce | flops 4096 | bytes 16384
  111.0 17.4 %all-gather.2.cloned.1.call-done = bf16[4096,1376]{0,1:T(8,128)(2,1)} async-done(((bf16[256,1376]{0,1:T(8,128)(2,1)}), bf16[4096,1376]{0,1:T(8,128)(2,1)}) %all-gather.2.cloned.1.call-update) | async-done | bytes 11272208 | tf_op jit(solution)/shard_map/all_gather | solution.py:23
  128.5 10.5 %fusion = (bf16[4096,688]{0,1:T(8,128)(2,1)}, bf16[4096,688]{0,1:T(8,128)(2,1)}) fusion(bf16[4096,1376]{0,1:T(8,128)(2,1)} %all-gather.2.cloned.1.call-done), kind=kLoop, calls=%fused_computation.8 | loop fusion | bytes 22544384 | tf_op jit(solution)/shard_map/slice | solution.py:25
  138.9 0.0 copy-done
  138.9 0.0 copy-done.1
  138.9 0.0 copy-done.2
  138.9 0.0 copy-done.3
  (4 shorter events, 0.0 us)
Async XLA Ops:
  7.2 23.6 %copy-start.4 = (f32[16]{0:T(128)S(1)}, f32[16]{0:T(128)}, u32[]{:S(2)}) copy-start(f32[16]{0:T(128)} %param.14) | copy-start | bytes 196
  7.2 23.6 %copy-start.5 = (f32[16]{0:T(128)S(1)}, f32[16]{0:T(128)}, u32[]{:S(2)}) copy-start(f32[16]{0:T(128)} %param.15) | copy-start | bytes 196
  7.2 121.3 %all-gather.2.cloned.1.call-start = ((), (), s32[]{:S(2)}) async-start(), calls=%async_computation | async-start | bytes 11976704 | tf_op jit(solution)/shard_map/all_gather | solution.py:23
  9.8 129.2 %copy-start = (f32[256,688]{0,1:T(8,128)}, f32[256,688]{0,1:T(8,128)S(1)}, u32[]{:S(2)}) copy-start(f32[256,688]{0,1:T(8,128)S(1)} %get-tuple-element.14) | copy-start | bytes 2113540
  9.8 129.2 %copy-start.1 = (f32[256,688]{0,1:T(8,128)}, f32[256,688]{0,1:T(8,128)S(1)}, u32[]{:S(2)}) copy-start(f32[256,688]{0,1:T(8,128)S(1)} %get-tuple-element.18) | copy-start | bytes 2113540
  29.5 109.4 %copy-start.2 = (f32[688]{0:T(1024)}, f32[688]{0:T(1024)S(1)}, u32[]{:S(2)}) copy-start(f32[688]{0:T(1024)S(1)} %sqrt.6) | copy-start | bytes 8260
  29.5 109.4 %copy-start.3 = (f32[688]{0:T(1024)}, f32[688]{0:T(1024)S(1)}, u32[]{:S(2)}) copy-start(f32[688]{0:T(1024)S(1)} %sqrt.7) | copy-start | bytes 8260
Sparse Core Ops, SparseCore 0:
  30.9 97.5 all-gather.1
where the time goes:
time: 146 us
  blocking collectives  99.6 us (68%)
  waiting for transfers between devices  17.4 us (12%)
  between operations  14.2 us (10%)
  local copies, waits for them, and re-layouts  10.8 us (7%)
  other arithmetic  3.76 us (3%)
    unnamed x1, blocking collectives  80 us
    psum x2, blocking collectives, one_axis_at_a_time(): array = lax.psum(array, axis)  19.7 us
    all_gather x1, waiting for transfers between devices, side_by_side(): result, at, done = (lax.all_gather(both, axis, axis=dim, tiled=True), 0, [])  17.4 us
    slice x1, local copies, waits for them, and re-layouts, side_by_side(): done.append(lax.slice_in_dim(result, at, at + a.shape[along], axis=along))  10.5 us
  transfers between devices with their start and end apart: 1, of which 1 were waited for; matrix products, arithmetic and copies ran while one was open for 0% of the time, Pallas kernels for 0%

commit v1 on v0

v1 whole, which is shorter than its diff:
```python
import jax
import jax.numpy as jnp
from jax import lax
from jax.experimental import pallas as pl
from jax.experimental.pallas import tpu as pltpu
from jax.sharding import Mesh
from jax.sharding import PartitionSpec as P

Y, X, W = "fsdp_0", "fsdp_1", "width"
FSDP = (Y, X)
FSDP_WIDTH = (Y, X, W)

learn_rate = 0.3
hold_rate = 0.9


def shift(array, axis, by):
    n = lax.axis_size(axis)
    return lax.ppermute(array, axis, [(i, (i + by) % n) for i in range(n)])


def swap(array, axis):
    return lax.ppermute(array, axis, [(i, i ^ 1) for i in range(lax.axis_size(axis))])


def spread(own, first, second):
    n = own.shape[0]
    h = n // 2
    right, left = shift(own, first, 1), shift(own, first, -1)
    up, down = shift(own, second, 1), shift(own, second, -1)
    right2 = shift(right[:h], first, 1)
    left2 = shift(left[h:], first, -1)
    near = jnp.concatenate([right, left])
    near_up, near_down = shift(near, second, 1), shift(near, second, -1)
    far = jnp.concatenate([right2, left2])
    far_up, far_down = shift(far, second, 1), shift(far, second, -1)
    up2 = shift(jnp.concatenate([up[:h], near_up[:n]]), second, 1)
    down2 = shift(jnp.concatenate([down[h:], near_down[n:]]), second, -1)
    far_up2 = shift(far_up[:h], second, 1)
    far_down2 = shift(far_down[h:], second, -1)
    return [
        (0, 0, 0, n, own, 0),
        (1, 0, 0, n, near, 0),
        (3, 0, 0, n, near, n),
        (2, 0, 0, n, far, 0),
        (0, 1, 0, n, up, 0),
        (0, 3, 0, n, down, 0),
        (1, 1, 0, n, near_up, 0),
        (3, 1, 0, n, near_up, n),
        (1, 3, 0, n, near_down, 0),
        (3, 3, 0, n, near_down, n),
        (2, 1, 0, n, far_up, 0),
        (2, 3, 0, n, far_down, 0),
    ], [
        (0, 2, 0, h, up2, 0),
        (1, 2, 0, n, up2, h),
        (0, 2, h, h, down2, 0),
        (3, 2, 0, n, down2, h),
        (2, 2, 0, h, far_up2, 0),
        (2, 2, h, h, far_down2, 0),
    ]


def place(plans, shapes, begun):
    arrays, moves = [], []
    for out, (plan, swapped) in enumerate(plans):
        for back1, back2, row, rows, array, start in plan:
            for k, a in enumerate(arrays):
                if a is array:
                    break
            else:
                k = len(arrays)
                arrays.append(array)
            dy, dx = (back1, back2) if swapped else (back2, back1)
            moves.append((out, dy, dx, row, rows, k, start))
    n_in = len(arrays)

    def body(*refs):
        y, x = lax.axis_index(Y), lax.axis_index(X)
        ins, outs, sem = refs[:n_in], refs[n_in + len(begun) : -1], refs[-1]
        copies = []
        for out, dy, dx, row, rows, k, start in moves:
            lane = lax.rem(y + 4 - dy, 4) * 1024 + lax.rem(x + 4 - dx, 4) * 256
            lane = pl.multiple_of(lane, 256)
            c = pltpu.make_async_copy(
                ins[k].at[pl.ds(start, rows), :],
                outs[out].at[pl.ds(row, rows), pl.ds(lane, 256)],
                sem.at[len(copies)],
            )
            c.start()
            copies.append(c)
        for c in copies:
            c.wait()

    return pl.pallas_call(
        body,
        out_shape=[jax.ShapeDtypeStruct(s, jnp.bfloat16) for s in shapes],
        in_specs=[pl.BlockSpec(memory_space=pl.ANY)] * (n_in + len(begun)),
        out_specs=[pl.BlockSpec(memory_space=pl.ANY)] * len(shapes),
        scratch_shapes=[pltpu.SemaphoreType.DMA((len(moves),))],
        input_output_aliases={n_in + k: k for k in range(len(begun))},
        compiler_params=pltpu.CompilerParams(vmem_limit_bytes=1 << 20),
    )(*(pltpu.with_memory_space_constraint(a, pltpu.VMEM) for a in arrays), *begun)


def shards(
    train_gate, drift_gate, spread_gate, train_up, drift_up, spread_up, norm_train, norm_step
):
    whole_gate = train_gate - learn_rate * (hold_rate * drift_gate + spread_gate)
    whole_up = train_up - learn_rate * (hold_rate * drift_up + spread_up)
    n = whole_gate.shape[1]
    width = lax.axis_size(W)
    squares = (jnp.sum(whole_gate * whole_gate, axis=0), jnp.sum(whole_up * whole_up, axis=0))
    squares, norm_train, norm_step = lax.optimization_barrier((squares, norm_train, norm_step))
    norm = (norm_train + norm_step).astype(jnp.bfloat16).astype(jnp.float32)
    mine = lax.broadcasted_iota(jnp.int32, (width, 1), 0) == lax.axis_index(W)
    norm = jnp.where(mine, norm, 0.0).reshape(-1)
    fill = -2 * n % 128
    told = jnp.concatenate(
        [
            *squares,
            jnp.zeros((fill,), jnp.float32),
            norm,
        ]
    ).reshape(-1, 128)
    heard = lax.all_to_all(
        jnp.broadcast_to(told[None], (16,) + told.shape), FSDP, 0, 0, tiled=True
    )
    last = (2 * n + fill) // 128
    total = jnp.sum(heard[:, :last], axis=0).reshape(-1)
    scale_gate, scale_up = jnp.sqrt(total[:n]), jnp.sqrt(total[n : 2 * n])
    narrow_gate = (whole_gate / scale_gate).astype(jnp.bfloat16).T
    narrow_up = (whole_up / scale_up).astype(jnp.bfloat16).T

    gate_first, gate_last = spread(narrow_gate, X, Y)
    up_first, up_last = spread(narrow_up, Y, X)
    shapes = [(n, 16 * narrow_gate.shape[1])] * 2
    begun = place([(gate_first, False), (up_first, True)], shapes, [])
    serving_gate, serving_up = place([(gate_last, False), (up_last, True)], shapes, begun)

    norms = heard[:, last:].astype(jnp.bfloat16).reshape(-1, 128)
    by, step = 1, 0
    while by < width:
        step += 1
        more = shift(norms, W, by) if by > 1 else swap(norms, W)
        norms = norms + more
        by *= 2
    norms = norms.reshape(-1)
    return (serving_gate.T, serving_up.T, scale_gate, scale_up, norms, whole_gate, whole_up)


def solution(mesh):
    split = Mesh(mesh.devices.reshape(4, 4, mesh.shape["width"]), (Y, X, W))
    weight, gain = P(FSDP, W), P(FSDP_WIDTH)
    return jax.shard_map(
        shards,
        mesh=split,
        in_specs=(weight,) * 6 + (gain,) * 2,
        out_specs=(P(None, W), P(None, W), P(W), P(W), P(), weight, weight),
        check_vma=False,
    )
```

time: 146 us -> 120 us (0.82)
  blocking collectives: 99.6 us -> 13.9 us
  starting transfers between devices: 0.04 us -> 44.8 us
  waiting for transfers between devices: 17.4 us -> 48.6 us
  between operations: 14.2 us -> 1.32 us
  local copies, waits for them, and re-layouts: 10.8 us -> 1.51 us
  Pallas kernels: 0 us -> 5.19 us
    unnamed x1 -> x0, blocking collectives: 80 us -> none
    ppermute x0 -> x32, waiting for transfers between devices: none -> 48.6 us  [the longest x31 47.4 us: shift(): return lax.ppermute(array, axis, [(i, (i + by) % n) for i in range(n)])]
    ppermute x0 -> x32, starting transfers between devices: none -> 44.8 us  [the longest x31 44.7 us: shift(): return lax.ppermute(array, axis, [(i, (i + by) % n) for i in range(n)])]
    psum x2 -> x0, blocking collectives: 19.7 us -> none  [one_axis_at_a_time(): array = lax.psum(array, axis)]
    all_gather x1 -> x0, waiting for transfers between devices: 17.4 us -> none  [side_by_side(): result, at, done = (lax.all_gather(both, axis, axis=dim, tiled=True), 0, [])]
    all_to_all x0 -> x1, blocking collectives: none -> 13.9 us  [shards(): lax.all_to_all(jnp.broadcast_to(told[None], (16,) + told.shape), FSDP, 0,...]
    slice x1 -> x21, local copies, waits for them, and re-layouts: 10.5 us -> 1.04 us  [the longest x6 0.87 us: spread(): down2 = shift(jnp.concatenate([down[h:], near_down[n:]]), second, -1)]
    pallas_call x0 -> x2, Pallas kernels: none -> 5.19 us  [place(): pl.pallas_call(body, out_shape=[jax.ShapeDtypeStruct(s, jnp.bfloat16) for...]
  transfers between devices with their start and end apart: 1 -> 32, of which waited for: 1 -> 12; matrix products, arithmetic and copies ran while one was open for 0% -> 1% of each run, Pallas kernels for 0% -> 3%
where the time goes in v1:
time: 120 us; the launch traced here: 119 us
  waiting for transfers between devices  48.6 us (40%)
  starting transfers between devices  44.8 us (37%)
  blocking collectives  13.9 us (12%)
  Pallas kernels  5.19 us (4%)
  other arithmetic  3.73 us (3%)
  local copies, waits for them, and re-layouts  1.51 us (1%)
  between operations  1.32 us (1%)
    ppermute x31, waiting for transfers between devices, shift(): return lax.ppermute(array, axis, [(i, (i + by) % n) for i in range(n)])  47.4 us
    ppermute x31, starting transfers between devices, shift(): return lax.ppermute(array, axis, [(i, (i + by) % n) for i in range(n)])  44.7 us
    all_to_all x1, blocking collectives, shards(): lax.all_to_all(jnp.broadcast_to(told[None], (16,) + told.shape), FSDP, 0,...  13.9 us
    pallas_call x2, Pallas kernels, place(): pl.pallas_call(body, out_shape=[jax.ShapeDtypeStruct(s, jnp.bfloat16) for...  5.19 us
    reduce_sum x1, other arithmetic, shards(): jnp.sum(whole_up * whole_up, axis=0)  2.53 us
  transfers between devices with their start and end apart: 32, of which 12 were waited for; matrix products, arithmetic and copies ran while one was open for 1% of the time, Pallas kernels for 3%

profile of v1, /device:TPU:2, one launch (start us, length us, event | category | flops | bytes accessed | tf_op | source)
XLA Modules:
  0.0 119.0 jit_solution(3493673959371908733)
XLA Ops:
  0.7 2.5 %multiply_reduce_fusion = (f32[688]{0:T(1024)S(1)}, f32[256,688]{0,1:T(8,128)S(1)}, f32[688]{0:T(1024)S(1)}, f32[256,688]{0,1:T(8,128)S(1)}) fusion(f32[256,688]{0,1:T(8,128)} %param.11, f32[256,688]{0,1:T(8,128)} %param.13, f32[256,688]{0,1:T(8,128)} %param.12, f32[256,688]{0,1:T(8,128)} %param.8, f32[256,688]{0,1:T(8,128)} %param.10, f32[256,688]{0,1:T(8,128)} %param.9), kind=kLoop, calls=%fused_computation.2 | loop fusion | flops 2112160 | bytes 5641600 | tf_op jit(solution)/shard_map/reduce_sum | solution.py:113
  3.5 13.9 %all_to_all.5 = f32[16,13,128]{2,1,0:T(8,128)S(1)} all-to-all(f32[16,13,128]{2,1,0:T(8,128)S(1)} %broadcast_in_dim.33), channel_id=1, replica_groups=mesh['fsdp_0'=4,'fsdp_1'=4,'width'=16] {'fsdp_0','fsdp_1'}, dimensions={0} | all-to-all | bytes 212992 | tf_op jit(solution)/shard_map/all_to_all | solution.py:126
  17.7 1.5 %collective-permute-start.2 = (bf16[688,256]{1,0:T(8,128)(2,1)S(1)}, bf16[688,256]{1,0:T(8,128)(2,1)S(1)}, u32[]{:S(2)}, u32[]{:S(2)}) collective-permute-start(bf16[688,256]{1,0:T(8,128)(2,1)S(1)} %fusion.refs_0_), channel_id=1, source_target_pairs={{0,48},{16,0},{32,16},{48,32},{1,49},{17,1},{33,17},{49,33},{2,50}... | collective-permute-start | bytes 1056776 | tf_op jit(solution)/shard_map/ppermute | solution.py:19
  20.3 3.0 %collective-permute-start.16 = (bf16[688,256]{1,0:T(8,128)(2,1)S(1)}, bf16[688,256]{1,0:T(8,128)(2,1)S(1)}, u32[]{:S(2)}, u32[]{:S(2)}) collective-permute-start(bf16[688,256]{1,0:T(8,128)(2,1)S(1)} %fusion.1.refs_9_), channel_id=1, source_target_pairs={{0,192},{64,0},{128,64},{192,128},{1,193},{65,1},{129,65},{193,129... | collective-permute-start | bytes 1056776 | tf_op jit(solution)/shard_map/ppermute | solution.py:19
  24.6 1.9 %collective-permute-start.29 = (bf16[32,128]{1,0:T(8,128)(2,1)S(1)}, bf16[32,128]{1,0:T(8,128)(2,1)S(1)}, u32[]{:S(2)}, u32[]{:S(2)}) collective-permute-start(bf16[32,128]{1,0:T(8,128)(2,1)S(1)} %add.24), channel_id=1, source_target_pairs={{0,2},{1,3},{2,4},{3,5},{4,6},{5,7},{6,8},{7,9},{8,10},{9,11},{10,... | collective-permute-start | bytes 24584 | tf_op jit(solution)/shard_map/ppermute | solution.py:19
  26.5 5.6 %collective-permute-done.29 = bf16[32,128]{1,0:T(8,128)(2,1)S(1)} collective-permute-done((bf16[32,128]{1,0:T(8,128)(2,1)S(1)}, bf16[32,128]{1,0:T(8,128)(2,1)S(1)}, u32[]{:S(2)}, u32[]{:S(2)}) %collective-permute-start.29) | collective-permute-done | bytes 8224 | tf_op jit(solution)/shard_map/ppermute | solution.py:19
  32.1 2.1 %collective-permute-start = (bf16[688,256]{1,0:T(8,128)(2,1)S(1)}, bf16[688,256]{1,0:T(8,128)(2,1)S(1)}, u32[]{:S(2)}, u32[]{:S(2)}) collective-permute-start(bf16[688,256]{1,0:T(8,128)(2,1)S(1)} %fusion.refs_0_), channel_id=1, source_target_pairs={{0,64},{64,128},{128,192},{192,0},{1,65},{65,129},{129,193},{193,1... | collective-permute-start | bytes 1056776 | tf_op jit(solution)/shard_map/ppermute | solution.py:19
  36.6 5.7 %collective-permute-done.30 = bf16[32,128]{1,0:T(8,128)(2,1)S(1)} collective-permute-done((bf16[32,128]{1,0:T(8,128)(2,1)S(1)}, bf16[32,128]{1,0:T(8,128)(2,1)S(1)}, u32[]{:S(2)}, u32[]{:S(2)}) %collective-permute-start.30) | collective-permute-done | bytes 8224 | tf_op jit(solution)/shard_map/ppermute | solution.py:19
  42.2 1.6 %collective-permute-start.20 = (bf16[1376,256]{1,0:T(8,128)(2,1)S(1)}, bf16[1376,256]{1,0:T(8,128)(2,1)S(1)}, u32[]{:S(2)}, u32[]{:S(2)}) collective-permute-start(bf16[1376,256]{1,0:T(8,128)(2,1)S(1)} %constant_dynamic-update-slice_fusion.4.refs_10_), channel_id=1, source_target_pairs={{0,48},{16,0},{32,16},{48,32},{1,49},{17,1},{33,17},{49,33},{2,50}... | collective-permute-start | bytes 2113544 | tf_op jit(solution)/shard_map/ppermute | solution.py:19
  44.3 2.9 %collective-permute-start.9 = (bf16[344,256]{1,0:T(8,128)(2,1)S(1)}, bf16[344,256]{1,0:T(8,128)(2,1)S(1)}, u32[]{:S(2)}, u32[]{:S(2)}) collective-permute-start(bf16[344,256]{1,0:T(8,128)(2,1)S(1)} %slice.88), channel_id=1, source_target_pairs={{0,48},{16,0},{32,16},{48,32},{1,49},{17,1},{33,17},{49,33},{2,50}... | collective-permute-start | bytes 528392 | tf_op jit(solution)/shard_map/ppermute | solution.py:19
  48.6 13.4 %collective-permute-done.9 = bf16[344,256]{1,0:T(8,128)(2,1)S(1)} collective-permute-done((bf16[344,256]{1,0:T(8,128)(2,1)S(1)}, bf16[344,256]{1,0:T(8,128)(2,1)S(1)}, u32[]{:S(2)}, u32[]{:S(2)}) %collective-permute-start.9) | collective-permute-done | bytes 176160 | tf_op jit(solution)/shard_map/ppermute | solution.py:19
  64.1 4.4 %collective-permute-done.23 = bf16[344,256]{1,0:T(8,128)(2,1)S(1)} collective-permute-done((bf16[344,256]{1,0:T(8,128)(2,1)S(1)}, bf16[344,256]{1,0:T(8,128)(2,1)S(1)}, u32[]{:S(2)}, u32[]{:S(2)}) %collective-permute-start.23) | collective-permute-done | bytes 176160 | tf_op jit(solution)/shard_map/ppermute | solution.py:19
  68.4 1.7 %collective-permute-start.12 = (bf16[688,256]{1,0:T(8,128)(2,1)S(1)}, bf16[688,256]{1,0:T(8,128)(2,1)S(1)}, u32[]{:S(2)}, u32[]{:S(2)}) collective-permute-start(bf16[688,256]{1,0:T(8,128)(2,1)S(1)} %constant_dynamic-update-slice_fusion.2.refs_2_), channel_id=1, source_target_pairs={{0,192},{64,0},{128,64},{192,128},{1,193},{65,1},{129,65},{193,129... | collective-permute-start | bytes 1056776 | tf_op jit(solution)/shard_map/ppermute | solution.py:19
  70.6 5.2 %collective-permute-done.12.refs_8_ = bf16[688,256]{1,0:T(8,128)(2,1)S(1)} collective-permute-done((bf16[688,256]{1,0:T(8,128)(2,1)S(1)}, bf16[688,256]{1,0:T(8,128)(2,1)S(1)}, u32[]{:S(2)}, u32[]{:S(2)}) %collective-permute-start.12) | collective-permute-done | bytes 352288 | tf_op jit(solution)/shard_map/ppermute | solution.py:19
  75.8 4.6 %collective-permute-start.31 = (bf16[32,128]{1,0:T(8,128)(2,1)S(1)}, bf16[32,128]{1,0:T(8,128)(2,1)S(1)}, u32[]{:S(2)}, u32[]{:S(2)}) collective-permute-start(bf16[32,128]{1,0:T(8,128)(2,1)S(1)} %add.26), channel_id=1, source_target_pairs={{0,8},{1,9},{2,10},{3,11},{4,12},{5,13},{6,14},{7,15},{8,0},{9,1},... | collective-permute-start | bytes 24584 | tf_op jit(solution)/shard_map/ppermute | solution.py:19
  80.7 3.7 %collective-permute-start.26 = (bf16[688,256]{1,0:T(8,128)(2,1)S(1)}, bf16[688,256]{1,0:T(8,128)(2,1)S(1)}, u32[]{:S(2)}, u32[]{:S(2)}) collective-permute-start(bf16[688,256]{1,0:T(8,128)(2,1)S(1)} %constant_dynamic-update-slice_fusion.6.refs_11_), channel_id=1, source_target_pairs={{0,48},{16,0},{32,16},{48,32},{1,49},{17,1},{33,17},{49,33},{2,50}... | collective-permute-start | bytes 1056776 | tf_op jit(solution)/shard_map/ppermute | solution.py:19
  84.6 3.3 %collective-permute-start.13 = (bf16[344,256]{1,0:T(8,128)(2,1)S(1)}, bf16[344,256]{1,0:T(8,128)(2,1)S(1)}, u32[]{:S(2)}, u32[]{:S(2)}) collective-permute-start(bf16[344,256]{1,0:T(8,128)(2,1)S(1)} %slice.90), channel_id=1, source_target_pairs={{0,192},{64,0},{128,64},{192,128},{1,193},{65,1},{129,65},{193,129... | collective-permute-start | bytes 528392 | tf_op jit(solution)/shard_map/ppermute | solution.py:19
  88.9 7.5 %collective-permute-done.3.refs_5_ = bf16[1376,256]{1,0:T(8,128)(2,1)S(1)} collective-permute-done((bf16[1376,256]{1,0:T(8,128)(2,1)S(1)}, bf16[1376,256]{1,0:T(8,128)(2,1)S(1)}, u32[]{:S(2)}, u32[]{:S(2)}) %collective-permute-start.3) | collective-permute-done | bytes 704544 | tf_op jit(solution)/shard_map/ppermute | solution.py:19
  96.5 3.6 %collective-permute-start.21 = (bf16[1032,256]{1,0:T(8,128)(2,1)S(1)}, bf16[1032,256]{1,0:T(8,128)(2,1)S(1)}, u32[]{:S(2)}, u32[]{:S(2)}) collective-permute-start(bf16[1032,256]{1,0:T(8,128)(2,1)S(1)} %pad_maximum_fusion.3), channel_id=1, source_target_pairs={{0,48},{16,0},{32,16},{48,32},{1,49},{17,1},{33,17},{49,33},{2,50}... | collective-permute-start | bytes 1585160 | tf_op jit(solution)/shard_map/ppermute | solution.py:19
  100.0 3.3 %collective-permute-start.7 = (bf16[1032,256]{1,0:T(8,128)(2,1)S(1)}, bf16[1032,256]{1,0:T(8,128)(2,1)S(1)}, u32[]{:S(2)}, u32[]{:S(2)}) collective-permute-start(bf16[1032,256]{1,0:T(8,128)(2,1)S(1)} %pad_maximum_fusion.1), channel_id=1, source_target_pairs={{0,192},{64,0},{128,64},{192,128},{1,193},{65,1},{129,65},{193,129... | collective-permute-start | bytes 1585160 | tf_op jit(solution)/shard_map/ppermute | solution.py:19
  104.9 3.4 %collective-permute-start.27 = (bf16[344,256]{1,0:T(8,128)(2,1)S(1)}, bf16[344,256]{1,0:T(8,128)(2,1)S(1)}, u32[]{:S(2)}, u32[]{:S(2)}) collective-permute-start(bf16[344,256]{1,0:T(8,128)(2,1)S(1)} %slice.99), channel_id=1, source_target_pairs={{0,48},{16,0},{32,16},{48,32},{1,49},{17,1},{33,17},{49,33},{2,50}... | collective-permute-start | bytes 528392 | tf_op jit(solution)/shard_map/ppermute | solution.py:19
  108.2 3.0 %collective-permute-done.27.refs_7_ = bf16[344,256]{1,0:T(8,128)(2,1)S(1)} collective-permute-done((bf16[344,256]{1,0:T(8,128)(2,1)S(1)}, bf16[344,256]{1,0:T(8,128)(2,1)S(1)}, u32[]{:S(2)}, u32[]{:S(2)}) %collective-permute-start.27) | collective-permute-done | bytes 176160 | tf_op jit(solution)/shard_map/ppermute | solution.py:19
  112.9 3.5 %shard_map.135 = (bf16[688,4096]{1,0:T(8,128)(2,1)}, bf16[688,4096]{1,0:T(8,128)(2,1)}) custom-call(bf16[688,256]{1,0:T(8,128)(2,1)S(1)} %fusion.refs_0_, bf16[1376,256]{1,0:T(8,128)(2,1)S(1)} %constant_dynamic-update-slice_fusion.refs_1_, bf16[688,256]{1,0:T(8,128)(2,1)S(1)} %constant_dynamic-update-slice_fusion.2.refs_2_, bf16[688,256]{1,0:T(8,128)(2,1)S(1)} %copy-done.3, ...), custom_call_target="tpu_custom_call" | custom-call | tf_op jit(solution)/shard_map/pallas_call | solution.py:95
  117.1 1.7 %shard_map.136 = (bf16[688,4096]{1,0:T(8,128)(2,1)}, bf16[688,4096]{1,0:T(8,128)(2,1)}) custom-call(bf16[1032,256]{1,0:T(8,128)(2,1)S(1)} %collective-permute-done.4.refs_0_, bf16[1032,256]{1,0:T(8,128)(2,1)S(1)} %collective-permute-done.7.refs_1_, ...), custom_call_target="tpu_custom_call", output_to_operand_aliasing={{0}: (8, {}), {1}: (9, {})} | custom-call | tf_op jit(solution)/shard_map/pallas_call | solution.py:95
  (120 shorter events, 14.9 us)
Async XLA Ops:
  17.7 14.4 %collective-permute-start.2 = (bf16[688,256]{1,0:T(8,128)(2,1)S(1)}, bf16[688,256]{1,0:T(8,128)(2,1)S(1)}, u32[]{:S(2)}, u32[]{:S(2)}) collective-permute-start(bf16[688,256]{1,0:T(8,128)(2,1)S(1)} %fusion.refs_0_), channel_id=1, source_target_pairs={{0,48},{16,0},{32,16},{48,32},{1,49},{17,1},{33,17},{49,33},{2,50}... | collective-permute-start | bytes 1056776 | tf_op jit(solution)/shard_map/ppermute | solution.py:19
  19.2 15.0 %collective-permute-start.1 = (bf16[688,256]{1,0:T(8,128)(2,1)S(1)}, bf16[688,256]{1,0:T(8,128)(2,1)S(1)}, u32[]{:S(2)}, u32[]{:S(2)}) collective-permute-start(bf16[688,256]{1,0:T(8,128)(2,1)S(1)} %fusion.refs_0_), channel_id=1, source_target_pairs={{0,16},{16,32},{32,48},{48,0},{1,17},{17,33},{33,49},{49,1},{2,18}... | collective-permute-start | bytes 1056776 | tf_op jit(solution)/shard_map/ppermute | solution.py:19
  20.0 15.7 %collective-permute-start.15 = (bf16[688,256]{1,0:T(8,128)(2,1)S(1)}, bf16[688,256]{1,0:T(8,128)(2,1)S(1)}, u32[]{:S(2)}, u32[]{:S(2)}) collective-permute-start(bf16[688,256]{1,0:T(8,128)(2,1)S(1)} %fusion.1.refs_9_), channel_id=1, source_target_pairs={{0,64},{64,128},{128,192},{192,0},{1,65},{65,129},{129,193},{193,1... | collective-permute-start | bytes 1056776 | tf_op jit(solution)/shard_map/ppermute | solution.py:19
  20.3 16.0 %collective-permute-start.16 = (bf16[688,256]{1,0:T(8,128)(2,1)S(1)}, bf16[688,256]{1,0:T(8,128)(2,1)S(1)}, u32[]{:S(2)}, u32[]{:S(2)}) collective-permute-start(bf16[688,256]{1,0:T(8,128)(2,1)S(1)} %fusion.1.refs_9_), channel_id=1, source_target_pairs={{0,192},{64,0},{128,64},{192,128},{1,193},{65,1},{129,65},{193,129... | collective-permute-start | bytes 1056776 | tf_op jit(solution)/shard_map/ppermute | solution.py:19
  32.1 11.7 %collective-permute-start.5 = (bf16[688,256]{1,0:T(8,128)(2,1)S(1)}, bf16[688,256]{1,0:T(8,128)(2,1)S(1)}, u32[]{:S(2)}, u32[]{:S(2)}) collective-permute-start(bf16[688,256]{1,0:T(8,128)(2,1)S(1)} %fusion.refs_0_), channel_id=1, source_target_pairs={{0,192},{64,0},{128,64},{192,128},{1,193},{65,1},{129,65},{193,129... | collective-permute-start | bytes 1056776 | tf_op jit(solution)/shard_map/ppermute | solution.py:19
  32.1 12.2 %collective-permute-start = (bf16[688,256]{1,0:T(8,128)(2,1)S(1)}, bf16[688,256]{1,0:T(8,128)(2,1)S(1)}, u32[]{:S(2)}, u32[]{:S(2)}) collective-permute-start(bf16[688,256]{1,0:T(8,128)(2,1)S(1)} %fusion.refs_0_), channel_id=1, source_target_pairs={{0,64},{64,128},{128,192},{192,0},{1,65},{65,129},{129,193},{193,1... | collective-permute-start | bytes 1056776 | tf_op jit(solution)/shard_map/ppermute | solution.py:19
  34.2 12.9 %collective-permute-start.19 = (bf16[688,256]{1,0:T(8,128)(2,1)S(1)}, bf16[688,256]{1,0:T(8,128)(2,1)S(1)}, u32[]{:S(2)}, u32[]{:S(2)}) collective-permute-start(bf16[688,256]{1,0:T(8,128)(2,1)S(1)} %fusion.1.refs_9_), channel_id=1, source_target_pairs={{0,48},{16,0},{32,16},{48,32},{1,49},{17,1},{33,17},{49,33},{2,50}... | collective-permute-start | bytes 1056776 | tf_op jit(solution)/shard_map/ppermute | solution.py:19
  35.7 11.5 %collective-permute-start.14 = (bf16[688,256]{1,0:T(8,128)(2,1)S(1)}, bf16[688,256]{1,0:T(8,128)(2,1)S(1)}, u32[]{:S(2)}, u32[]{:S(2)}) collective-permute-start(bf16[688,256]{1,0:T(8,128)(2,1)S(1)} %fusion.1.refs_9_), channel_id=1, source_target_pairs={{0,16},{16,32},{32,48},{48,0},{1,17},{17,33},{33,49},{49,1},{2,18}... | collective-permute-start | bytes 1056776 | tf_op jit(solution)/shard_map/ppermute | solution.py:19
  42.2 38.5 %collective-permute-start.20 = (bf16[1376,256]{1,0:T(8,128)(2,1)S(1)}, bf16[1376,256]{1,0:T(8,128)(2,1)S(1)}, u32[]{:S(2)}, u32[]{:S(2)}) collective-permute-start(bf16[1376,256]{1,0:T(8,128)(2,1)S(1)} %constant_dynamic-update-slice_fusion.4.refs_10_), channel_id=1, source_target_pairs={{0,48},{16,0},{32,16},{48,32},{1,49},{17,1},{33,17},{49,33},{2,50}... | collective-permute-start | bytes 2113544 | tf_op jit(solution)/shard_map/ppermute | solution.py:19
  43.8 40.6 %collective-permute-start.17 = (bf16[1376,256]{1,0:T(8,128)(2,1)S(1)}, bf16[1376,256]{1,0:T(8,128)(2,1)S(1)}, u32[]{:S(2)}, u32[]{:S(2)}) collective-permute-start(bf16[1376,256]{1,0:T(8,128)(2,1)S(1)} %constant_dynamic-update-slice_fusion.4.refs_10_), channel_id=1, source_target_pairs={{0,16},{16,32},{32,48},{48,0},{1,17},{17,33},{33,49},{49,1},{2,18}... | collective-permute-start | bytes 2113544 | tf_op jit(solution)/shard_map/ppermute | solution.py:19
  44.3 17.7 %collective-permute-start.9 = (bf16[344,256]{1,0:T(8,128)(2,1)S(1)}, bf16[344,256]{1,0:T(8,128)(2,1)S(1)}, u32[]{:S(2)}, u32[]{:S(2)}) collective-permute-start(bf16[344,256]{1,0:T(8,128)(2,1)S(1)} %slice.88), channel_id=1, source_target_pairs={{0,48},{16,0},{32,16},{48,32},{1,49},{17,1},{33,17},{49,33},{2,50}... | collective-permute-start | bytes 528392 | tf_op jit(solution)/shard_map/ppermute | solution.py:19
  47.2 16.5 %collective-permute-start.8 = (bf16[344,256]{1,0:T(8,128)(2,1)S(1)}, bf16[344,256]{1,0:T(8,128)(2,1)S(1)}, u32[]{:S(2)}, u32[]{:S(2)}) collective-permute-start(bf16[344,256]{1,0:T(8,128)(2,1)S(1)} %slice.87), channel_id=1, source_target_pairs={{0,16},{16,32},{32,48},{48,0},{1,17},{17,33},{33,49},{49,1},{2,18}... | collective-permute-start | bytes 528392 | tf_op jit(solution)/shard_map/ppermute | solution.py:19
  47.2 37.3 %collective-permute-start.6 = (bf16[1376,256]{1,0:T(8,128)(2,1)S(1)}, bf16[1376,256]{1,0:T(8,128)(2,1)S(1)}, u32[]{:S(2)}, u32[]{:S(2)}) collective-permute-start(bf16[1376,256]{1,0:T(8,128)(2,1)S(1)} %constant_dynamic-update-slice_fusion.refs_1_), channel_id=1, source_target_pairs={{0,192},{64,0},{128,64},{192,128},{1,193},{65,1},{129,65},{193,129... | collective-permute-start | bytes 2113544 | tf_op jit(solution)/shard_map/ppermute | solution.py:19
  70.4 10.0 %collective-permute-start.10 = (bf16[688,256]{1,0:T(8,128)(2,1)S(1)}, bf16[688,256]{1,0:T(8,128)(2,1)S(1)}, u32[]{:S(2)}, u32[]{:S(2)}) collective-permute-start(bf16[688,256]{1,0:T(8,128)(2,1)S(1)} %constant_dynamic-update-slice_fusion.2.refs_2_), channel_id=1, source_target_pairs={{0,64},{64,128},{128,192},{192,0},{1,65},{65,129},{129,193},{193,1... | collective-permute-start | bytes 1056776 | tf_op jit(solution)/shard_map/ppermute | solution.py:19
  75.8 20.7 %collective-permute-start.31 = (bf16[32,128]{1,0:T(8,128)(2,1)S(1)}, bf16[32,128]{1,0:T(8,128)(2,1)S(1)}, u32[]{:S(2)}, u32[]{:S(2)}) collective-permute-start(bf16[32,128]{1,0:T(8,128)(2,1)S(1)} %add.26), channel_id=1, source_target_pairs={{0,8},{1,9},{2,10},{3,11},{4,12},{5,13},{6,14},{7,15},{8,0},{9,1},... | collective-permute-start | bytes 24584 | tf_op jit(solution)/shard_map/ppermute | solution.py:19
  80.4 15.9 %collective-permute-start.3 = (bf16[1376,256]{1,0:T(8,128)(2,1)S(1)}, bf16[1376,256]{1,0:T(8,128)(2,1)S(1)}, u32[]{:S(2)}, u32[]{:S(2)}) collective-permute-start(bf16[1376,256]{1,0:T(8,128)(2,1)S(1)} %constant_dynamic-update-slice_fusion.refs_1_), channel_id=1, source_target_pairs={{0,64},{64,128},{128,192},{192,0},{1,65},{65,129},{129,193},{193,1... | collective-permute-start | bytes 2113544 | tf_op jit(solution)/shard_map/ppermute | solution.py:19
  80.7 19.3 %collective-permute-start.26 = (bf16[688,256]{1,0:T(8,128)(2,1)S(1)}, bf16[688,256]{1,0:T(8,128)(2,1)S(1)}, u32[]{:S(2)}, u32[]{:S(2)}) collective-permute-start(bf16[688,256]{1,0:T(8,128)(2,1)S(1)} %constant_dynamic-update-slice_fusion.6.refs_11_), channel_id=1, source_target_pairs={{0,48},{16,0},{32,16},{48,32},{1,49},{17,1},{33,17},{49,33},{2,50}... | collective-permute-start | bytes 1056776 | tf_op jit(solution)/shard_map/ppermute | solution.py:19
  84.4 15.6 %collective-permute-start.24 = (bf16[688,256]{1,0:T(8,128)(2,1)S(1)}, bf16[688,256]{1,0:T(8,128)(2,1)S(1)}, u32[]{:S(2)}, u32[]{:S(2)}) collective-permute-start(bf16[688,256]{1,0:T(8,128)(2,1)S(1)} %constant_dynamic-update-slice_fusion.6.refs_11_), channel_id=1, source_target_pairs={{0,16},{16,32},{32,48},{48,0},{1,17},{17,33},{33,49},{49,1},{2,18}... | collective-permute-start | bytes 1056776 | tf_op jit(solution)/shard_map/ppermute | solution.py:19
  84.6 18.8 %collective-permute-start.13 = (bf16[344,256]{1,0:T(8,128)(2,1)S(1)}, bf16[344,256]{1,0:T(8,128)(2,1)S(1)}, u32[]{:S(2)}, u32[]{:S(2)}) collective-permute-start(bf16[344,256]{1,0:T(8,128)(2,1)S(1)} %slice.90), channel_id=1, source_target_pairs={{0,192},{64,0},{128,64},{192,128},{1,193},{65,1},{129,65},{193,129... | collective-permute-start | bytes 528392 | tf_op jit(solution)/shard_map/ppermute | solution.py:19
  96.3 8.5 %collective-permute-start.11 = (bf16[344,256]{1,0:T(8,128)(2,1)S(1)}, bf16[344,256]{1,0:T(8,128)(2,1)S(1)}, u32[]{:S(2)}, u32[]{:S(2)}) collective-permute-start(bf16[344,256]{1,0:T(8,128)(2,1)S(1)} %slice.89), channel_id=1, source_target_pairs={{0,64},{64,128},{128,192},{192,0},{1,65},{65,129},{129,193},{193,1... | collective-permute-start | bytes 528392 | tf_op jit(solution)/shard_map/ppermute | solution.py:19
  96.5 20.6 %collective-permute-start.21 = (bf16[1032,256]{1,0:T(8,128)(2,1)S(1)}, bf16[1032,256]{1,0:T(8,128)(2,1)S(1)}, u32[]{:S(2)}, u32[]{:S(2)}) collective-permute-start(bf16[1032,256]{1,0:T(8,128)(2,1)S(1)} %pad_maximum_fusion.3), channel_id=1, source_target_pairs={{0,48},{16,0},{32,16},{48,32},{1,49},{17,1},{33,17},{49,33},{2,50}... | collective-permute-start | bytes 1585160 | tf_op jit(solution)/shard_map/ppermute | solution.py:19
  100.0 17.1 %collective-permute-start.18 = (bf16[1032,256]{1,0:T(8,128)(2,1)S(1)}, bf16[1032,256]{1,0:T(8,128)(2,1)S(1)}, u32[]{:S(2)}, u32[]{:S(2)}) collective-permute-start(bf16[1032,256]{1,0:T(8,128)(2,1)S(1)} %pad_maximum_fusion.2), channel_id=1, source_target_pairs={{0,16},{16,32},{32,48},{48,0},{1,17},{17,33},{33,49},{49,1},{2,18}... | collective-permute-start | bytes 1585160 | tf_op jit(solution)/shard_map/ppermute | solution.py:19
  100.0 17.1 %collective-permute-start.7 = (bf16[1032,256]{1,0:T(8,128)(2,1)S(1)}, bf16[1032,256]{1,0:T(8,128)(2,1)S(1)}, u32[]{:S(2)}, u32[]{:S(2)}) collective-permute-start(bf16[1032,256]{1,0:T(8,128)(2,1)S(1)} %pad_maximum_fusion.1), channel_id=1, source_target_pairs={{0,192},{64,0},{128,64},{192,128},{1,193},{65,1},{129,65},{193,129... | collective-permute-start | bytes 1585160 | tf_op jit(solution)/shard_map/ppermute | solution.py:19
  103.4 13.8 %collective-permute-start.4 = (bf16[1032,256]{1,0:T(8,128)(2,1)S(1)}, bf16[1032,256]{1,0:T(8,128)(2,1)S(1)}, u32[]{:S(2)}, u32[]{:S(2)}) collective-permute-start(bf16[1032,256]{1,0:T(8,128)(2,1)S(1)} %pad_maximum_fusion), channel_id=1, source_target_pairs={{0,64},{64,128},{128,192},{192,0},{1,65},{65,129},{129,193},{193,1... | collective-permute-start | bytes 1585160 | tf_op jit(solution)/shard_map/ppermute | solution.py:19
  (26 other events, 275.8 us)

commit v2 on v1

--- a/solution.py
+++ b/solution.py
@@ -56,6 +56,7 @@
         (1, 2, 0, n, up2, h),
         (0, 2, h, h, down2, 0),
         (3, 2, 0, n, down2, h),
+    ], [
         (2, 2, 0, h, far_up2, 0),
         (2, 2, h, h, far_down2, 0),
     ]
@@ -132,10 +133,11 @@
     narrow_gate = (whole_gate / scale_gate).astype(jnp.bfloat16).T
     narrow_up = (whole_up / scale_up).astype(jnp.bfloat16).T
 
-    gate_first, gate_last = spread(narrow_gate, X, Y)
-    up_first, up_last = spread(narrow_up, Y, X)
+    gate_first, gate_next, gate_last = spread(narrow_gate, X, Y)
+    up_first, up_next, up_last = spread(narrow_up, Y, X)
     shapes = [(n, 16 * narrow_gate.shape[1])] * 2
     begun = place([(gate_first, False), (up_first, True)], shapes, [])
+    begun = place([(gate_next, False), (up_next, True)], shapes, begun)
     serving_gate, serving_up = place([(gate_last, False), (up_last, True)], shapes, begun)
 
     norms = heard[:, last:].astype(jnp.bfloat16).reshape(-1, 128)

time: 120 us -> 123 us (1.025)
    ppermute x31, starting transfers between devices: 44.7 us -> 45.9 us  [shift(): return lax.ppermute(array, axis, [(i, (i + by) % n) for i in range(n)])]
    pallas_call x2 -> x3, Pallas kernels: 5.19 us -> 5.83 us  [place(): pl.pallas_call(body, out_shape=[jax.ShapeDtypeStruct(s, jnp.bfloat16) for...]
  transfers between devices with their start and end apart: 32 -> 32, of which waited for: 12 -> 14; matrix products, arithmetic and copies ran while one was open for 1% -> 1% of each run, Pallas kernels for 3% -> 4%
where the time goes in v2:
time: 123 us; the launch traced here: 121 us
  waiting for transfers between devices  48.6 us (40%)
  starting transfers between devices  46 us (37%)
  blocking collectives  13.9 us (11%)
  Pallas kernels  5.83 us (5%)
  other arithmetic  3.73 us (3%)
  local copies, waits for them, and re-layouts  2.08 us (2%)
  between operations  1.32 us (1%)
    ppermute x31, waiting for transfers between devices, shift(): return lax.ppermute(array, axis, [(i, (i + by) % n) for i in range(n)])  47.5 us
    ppermute x31, starting transfers between devices, shift(): return lax.ppermute(array, axis, [(i, (i + by) % n) for i in range(n)])  45.9 us
    all_to_all x1, blocking collectives, shards(): lax.all_to_all(jnp.broadcast_to(told[None], (16,) + told.shape), FSDP, 0,...  13.9 us
    pallas_call x3, Pallas kernels, place(): pl.pallas_call(body, out_shape=[jax.ShapeDtypeStruct(s, jnp.bfloat16) for...  5.83 us
    reduce_sum x1, other arithmetic, shards(): jnp.sum(whole_up * whole_up, axis=0)  2.53 us
  transfers between devices with their start and end apart: 32, of which 14 were waited for; matrix products, arithmetic and copies ran while one was open for 1% of the time, Pallas kernels for 4%

profile of v2, /device:TPU:2, one launch (start us, length us, event | category | flops | bytes accessed | tf_op | source)
XLA Modules:
  0.0 121.5 jit_solution(10935744828642733714)
XLA Ops:
  0.7 2.5 %multiply_reduce_fusion = (f32[688]{0:T(1024)S(1)}, f32[256,688]{0,1:T(8,128)S(1)}, f32[688]{0:T(1024)S(1)}, f32[256,688]{0,1:T(8,128)S(1)}) fusion(f32[256,688]{0,1:T(8,128)} %param.11, f32[256,688]{0,1:T(8,128)} %param.13, f32[256,688]{0,1:T(8,128)} %param.12, f32[256,688]{0,1:T(8,128)} %param.8, f32[256,688]{0,1:T(8,128)} %param.10, f32[256,688]{0,1:T(8,128)} %param.9), kind=kLoop, calls=%fused_computation.2 | loop fusion | flops 2112160 | bytes 5641600 | tf_op jit(solution)/shard_map/reduce_sum | solution.py:114
  3.5 13.9 %all_to_all.5 = f32[16,13,128]{2,1,0:T(8,128)S(1)} all-to-all(f32[16,13,128]{2,1,0:T(8,128)S(1)} %broadcast_in_dim.33), channel_id=1, replica_groups=mesh['fsdp_0'=4,'fsdp_1'=4,'width'=16] {'fsdp_0','fsdp_1'}, dimensions={0} | all-to-all | bytes 212992 | tf_op jit(solution)/shard_map/all_to_all | solution.py:127
  19.2 2.7 %collective-permute-start.10 = (bf16[688,256]{1,0:T(8,128)(2,1)S(1)}, bf16[688,256]{1,0:T(8,128)(2,1)S(1)}, u32[]{:S(2)}, u32[]{:S(2)}) collective-permute-start(bf16[688,256]{1,0:T(8,128)(2,1)S(1)} %fusion.1.refs_9_), channel_id=1, source_target_pairs={{0,192},{64,0},{128,64},{192,128},{1,193},{65,1},{129,65},{193,129... | collective-permute-start | bytes 1056776 | tf_op jit(solution)/shard_map/ppermute | solution.py:19
  23.2 1.9 %collective-permute-start.29 = (bf16[32,128]{1,0:T(8,128)(2,1)S(1)}, bf16[32,128]{1,0:T(8,128)(2,1)S(1)}, u32[]{:S(2)}, u32[]{:S(2)}) collective-permute-start(bf16[32,128]{1,0:T(8,128)(2,1)S(1)} %add.24), channel_id=1, source_target_pairs={{0,2},{1,3},{2,4},{3,5},{4,6},{5,7},{6,8},{7,9},{8,10},{9,11},{10,... | collective-permute-start | bytes 24584 | tf_op jit(solution)/shard_map/ppermute | solution.py:19
  25.1 5.6 %collective-permute-done.29 = bf16[32,128]{1,0:T(8,128)(2,1)S(1)} collective-permute-done((bf16[32,128]{1,0:T(8,128)(2,1)S(1)}, bf16[32,128]{1,0:T(8,128)(2,1)S(1)}, u32[]{:S(2)}, u32[]{:S(2)}) %collective-permute-start.29) | collective-permute-done | bytes 8224 | tf_op jit(solution)/shard_map/ppermute | solution.py:19
  32.1 2.7 %collective-permute-start.25 = (bf16[688,256]{1,0:T(8,128)(2,1)S(1)}, bf16[688,256]{1,0:T(8,128)(2,1)S(1)}, u32[]{:S(2)}, u32[]{:S(2)}) collective-permute-start(bf16[688,256]{1,0:T(8,128)(2,1)S(1)} %fusion.1.refs_9_), channel_id=1, source_target_pairs={{0,48},{16,0},{32,16},{48,32},{1,49},{17,1},{33,17},{49,33},{2,50}... | collective-permute-start | bytes 1056776 | tf_op jit(solution)/shard_map/ppermute | solution.py:19
  35.1 2.0 %collective-permute-start.26 = (bf16[1376,256]{1,0:T(8,128)(2,1)S(1)}, bf16[1376,256]{1,0:T(8,128)(2,1)S(1)}, u32[]{:S(2)}, u32[]{:S(2)}) collective-permute-start(bf16[1376,256]{1,0:T(8,128)(2,1)S(1)} %constant_dynamic-update-slice_fusion.6.refs_10_), channel_id=1, source_target_pairs={{0,48},{16,0},{32,16},{48,32},{1,49},{17,1},{33,17},{49,33},{2,50}... | collective-permute-start | bytes 2113544 | tf_op jit(solution)/shard_map/ppermute | solution.py:19
  37.1 4.2 %collective-permute-done.16.refs_3_ = bf16[688,256]{1,0:T(8,128)(2,1)S(1)} collective-permute-done((bf16[688,256]{1,0:T(8,128)(2,1)S(1)}, bf16[688,256]{1,0:T(8,128)(2,1)S(1)}, u32[]{:S(2)}, u32[]{:S(2)}) %collective-permute-start.16) | collective-permute-done | bytes 352288 | tf_op jit(solution)/shard_map/ppermute | solution.py:19
  42.5 2.3 %collective-permute-start.1 = (bf16[344,256]{1,0:T(8,128)(2,1)S(1)}, bf16[344,256]{1,0:T(8,128)(2,1)S(1)}, u32[]{:S(2)}, u32[]{:S(2)}) collective-permute-start(bf16[344,256]{1,0:T(8,128)(2,1)S(1)} %slice.83), channel_id=1, source_target_pairs={{0,16},{16,32},{32,48},{48,0},{1,17},{17,33},{33,49},{49,1},{2,18}... | collective-permute-start | bytes 528392 | tf_op jit(solution)/shard_map/ppermute | solution.py:19
  44.9 4.5 %collective-permute-done.25.refs_13_ = bf16[688,256]{1,0:T(8,128)(2,1)S(1)} collective-permute-done((bf16[688,256]{1,0:T(8,128)(2,1)S(1)}, bf16[688,256]{1,0:T(8,128)(2,1)S(1)}, u32[]{:S(2)}, u32[]{:S(2)}) %collective-permute-start.25) | collective-permute-done | bytes 352288 | tf_op jit(solution)/shard_map/ppermute | solution.py:19
  50.1 12.7 %collective-permute-done.1 = bf16[344,256]{1,0:T(8,128)(2,1)S(1)} collective-permute-done((bf16[344,256]{1,0:T(8,128)(2,1)S(1)}, bf16[344,256]{1,0:T(8,128)(2,1)S(1)}, u32[]{:S(2)}, u32[]{:S(2)}) %collective-permute-start.1) | collective-permute-done | bytes 176160 | tf_op jit(solution)/shard_map/ppermute | solution.py:19
  64.3 3.0 %collective-permute-start.11 = (bf16[344,256]{1,0:T(8,128)(2,1)S(1)}, bf16[344,256]{1,0:T(8,128)(2,1)S(1)}, u32[]{:S(2)}, u32[]{:S(2)}) collective-permute-start(bf16[344,256]{1,0:T(8,128)(2,1)S(1)} %slice.89), channel_id=1, source_target_pairs={{0,192},{64,0},{128,64},{192,128},{1,193},{65,1},{129,65},{193,129... | collective-permute-start | bytes 528392 | tf_op jit(solution)/shard_map/ppermute | solution.py:19
  68.2 3.0 %collective-permute-start.20 = (bf16[1376,256]{1,0:T(8,128)(2,1)S(1)}, bf16[1376,256]{1,0:T(8,128)(2,1)S(1)}, u32[]{:S(2)}, u32[]{:S(2)}) collective-permute-start(bf16[1376,256]{1,0:T(8,128)(2,1)S(1)} %constant_dynamic-update-slice_fusion.4.refs_1_), channel_id=1, source_target_pairs={{0,192},{64,0},{128,64},{192,128},{1,193},{65,1},{129,65},{193,129... | collective-permute-start | bytes 2113544 | tf_op jit(solution)/shard_map/ppermute | solution.py:19
  72.2 3.8 %collective-permute-start.6 = (bf16[688,256]{1,0:T(8,128)(2,1)S(1)}, bf16[688,256]{1,0:T(8,128)(2,1)S(1)}, u32[]{:S(2)}, u32[]{:S(2)}) collective-permute-start(bf16[688,256]{1,0:T(8,128)(2,1)S(1)} %constant_dynamic-update-slice_fusion.refs_2_), channel_id=1, source_target_pairs={{0,192},{64,0},{128,64},{192,128},{1,193},{65,1},{129,65},{193,129... | collective-permute-start | bytes 1056776 | tf_op jit(solution)/shard_map/ppermute | solution.py:19
  77.0 10.3 %collective-permute-done.20.refs_6_ = bf16[1376,256]{1,0:T(8,128)(2,1)S(1)} collective-permute-done((bf16[1376,256]{1,0:T(8,128)(2,1)S(1)}, bf16[1376,256]{1,0:T(8,128)(2,1)S(1)}, u32[]{:S(2)}, u32[]{:S(2)}) %collective-permute-start.20) | collective-permute-done | bytes 704544 | tf_op jit(solution)/shard_map/ppermute | solution.py:19
  90.1 1.5 %collective-permute-start.12 = (bf16[688,256]{1,0:T(8,128)(2,1)S(1)}, bf16[688,256]{1,0:T(8,128)(2,1)S(1)}, u32[]{:S(2)}, u32[]{:S(2)}) collective-permute-start(bf16[688,256]{1,0:T(8,128)(2,1)S(1)} %constant_dynamic-update-slice_fusion.2.refs_11_), channel_id=1, source_target_pairs={{0,16},{16,32},{32,48},{48,0},{1,17},{17,33},{33,49},{49,1},{2,18}... | collective-permute-start | bytes 1056776 | tf_op jit(solution)/shard_map/ppermute | solution.py:19
  92.5 2.0 %collective-permute-start.24 = (bf16[1032,256]{1,0:T(8,128)(2,1)S(1)}, bf16[1032,256]{1,0:T(8,128)(2,1)S(1)}, u32[]{:S(2)}, u32[]{:S(2)}) collective-permute-start(bf16[1032,256]{1,0:T(8,128)(2,1)S(1)} %pad_maximum_fusion.2), channel_id=1, source_target_pairs={{0,16},{16,32},{32,48},{48,0},{1,17},{17,33},{33,49},{49,1},{2,18}... | collective-permute-start | bytes 1585160 | tf_op jit(solution)/shard_map/ppermute | solution.py:19
  94.4 2.7 %collective-permute-start.21 = (bf16[1032,256]{1,0:T(8,128)(2,1)S(1)}, bf16[1032,256]{1,0:T(8,128)(2,1)S(1)}, u32[]{:S(2)}, u32[]{:S(2)}) collective-permute-start(bf16[1032,256]{1,0:T(8,128)(2,1)S(1)} %pad_maximum_fusion.1), channel_id=1, source_target_pairs={{0,192},{64,0},{128,64},{192,128},{1,193},{65,1},{129,65},{193,129... | collective-permute-start | bytes 1585160 | tf_op jit(solution)/shard_map/ppermute | solution.py:19
  98.4 2.8 %collective-permute-done.12.refs_16_ = bf16[688,256]{1,0:T(8,128)(2,1)S(1)} collective-permute-done((bf16[688,256]{1,0:T(8,128)(2,1)S(1)}, bf16[688,256]{1,0:T(8,128)(2,1)S(1)}, u32[]{:S(2)}, u32[]{:S(2)}) %collective-permute-start.12) | collective-permute-done | bytes 352288 | tf_op jit(solution)/shard_map/ppermute | solution.py:19
  101.3 4.6 %collective-permute-start.31 = (bf16[32,128]{1,0:T(8,128)(2,1)S(1)}, bf16[32,128]{1,0:T(8,128)(2,1)S(1)}, u32[]{:S(2)}, u32[]{:S(2)}) collective-permute-start(bf16[32,128]{1,0:T(8,128)(2,1)S(1)} %add.26), channel_id=1, source_target_pairs={{0,8},{1,9},{2,10},{3,11},{4,12},{5,13},{6,14},{7,15},{8,0},{9,1},... | collective-permute-start | bytes 24584 | tf_op jit(solution)/shard_map/ppermute | solution.py:19
  105.9 2.9 %collective-permute-done.31 = bf16[32,128]{1,0:T(8,128)(2,1)S(1)} collective-permute-done((bf16[32,128]{1,0:T(8,128)(2,1)S(1)}, bf16[32,128]{1,0:T(8,128)(2,1)S(1)}, u32[]{:S(2)}, u32[]{:S(2)}) %collective-permute-start.31) | collective-permute-done | bytes 8224 | tf_op jit(solution)/shard_map/ppermute | solution.py:19
  108.8 2.7 %collective-permute-start.7 = (bf16[344,256]{1,0:T(8,128)(2,1)S(1)}, bf16[344,256]{1,0:T(8,128)(2,1)S(1)}, u32[]{:S(2)}, u32[]{:S(2)}) collective-permute-start(bf16[344,256]{1,0:T(8,128)(2,1)S(1)} %slice.86), channel_id=1, source_target_pairs={{0,192},{64,0},{128,64},{192,128},{1,193},{65,1},{129,65},{193,129... | collective-permute-start | bytes 528392 | tf_op jit(solution)/shard_map/ppermute | solution.py:19
  111.5 3.3 %collective-permute-start.15 = (bf16[344,256]{1,0:T(8,128)(2,1)S(1)}, bf16[344,256]{1,0:T(8,128)(2,1)S(1)}, u32[]{:S(2)}, u32[]{:S(2)}) collective-permute-start(bf16[344,256]{1,0:T(8,128)(2,1)S(1)} %slice.91), channel_id=1, source_target_pairs={{0,48},{16,0},{32,16},{48,32},{1,49},{17,1},{33,17},{49,33},{2,50}... | collective-permute-start | bytes 528392 | tf_op jit(solution)/shard_map/ppermute | solution.py:19
  115.4 3.5 %shard_map.135 = (bf16[688,4096]{1,0:T(8,128)(2,1)}, bf16[688,4096]{1,0:T(8,128)(2,1)}) custom-call(bf16[688,256]{1,0:T(8,128)(2,1)S(1)} %fusion.refs_0_, bf16[1376,256]{1,0:T(8,128)(2,1)S(1)} %constant_dynamic-update-slice_fusion.4.refs_1_, bf16[688,256]{1,0:T(8,128)(2,1)S(1)} %constant_dynamic-update-slice_fusion.refs_2_, bf16[688,256]{1,0:T(8,128)(2,1)S(1)} %copy-done.3, ...), custom_call_target="tpu_custom_call" | custom-call | tf_op jit(solution)/shard_map/pallas_call | solution.py:96
  (121 shorter events, 19.2 us)
Async XLA Ops:
  17.7 13.0 %collective-permute-start = (bf16[688,256]{1,0:T(8,128)(2,1)S(1)}, bf16[688,256]{1,0:T(8,128)(2,1)S(1)}, u32[]{:S(2)}, u32[]{:S(2)}) collective-permute-start(bf16[688,256]{1,0:T(8,128)(2,1)S(1)} %fusion.refs_0_), channel_id=1, source_target_pairs={{0,16},{16,32},{32,48},{48,0},{1,17},{17,33},{33,49},{49,1},{2,18}... | collective-permute-start | bytes 1056776 | tf_op jit(solution)/shard_map/ppermute | solution.py:19
  18.6 13.5 %collective-permute-start.8 = (bf16[688,256]{1,0:T(8,128)(2,1)S(1)}, bf16[688,256]{1,0:T(8,128)(2,1)S(1)}, u32[]{:S(2)}, u32[]{:S(2)}) collective-permute-start(bf16[688,256]{1,0:T(8,128)(2,1)S(1)} %fusion.1.refs_9_), channel_id=1, source_target_pairs={{0,64},{64,128},{128,192},{192,0},{1,65},{65,129},{129,193},{193,1... | collective-permute-start | bytes 1056776 | tf_op jit(solution)/shard_map/ppermute | solution.py:19
  19.2 15.7 %collective-permute-start.10 = (bf16[688,256]{1,0:T(8,128)(2,1)S(1)}, bf16[688,256]{1,0:T(8,128)(2,1)S(1)}, u32[]{:S(2)}, u32[]{:S(2)}) collective-permute-start(bf16[688,256]{1,0:T(8,128)(2,1)S(1)} %fusion.1.refs_9_), channel_id=1, source_target_pairs={{0,192},{64,0},{128,64},{192,128},{1,193},{65,1},{129,65},{193,129... | collective-permute-start | bytes 1056776 | tf_op jit(solution)/shard_map/ppermute | solution.py:19
  25.1 10.0 %collective-permute-start.19 = (bf16[688,256]{1,0:T(8,128)(2,1)S(1)}, bf16[688,256]{1,0:T(8,128)(2,1)S(1)}, u32[]{:S(2)}, u32[]{:S(2)}) collective-permute-start(bf16[688,256]{1,0:T(8,128)(2,1)S(1)} %fusion.refs_0_), channel_id=1, source_target_pairs={{0,192},{64,0},{128,64},{192,128},{1,193},{65,1},{129,65},{193,129... | collective-permute-start | bytes 1056776 | tf_op jit(solution)/shard_map/ppermute | solution.py:19
  30.7 10.6 %collective-permute-start.16 = (bf16[688,256]{1,0:T(8,128)(2,1)S(1)}, bf16[688,256]{1,0:T(8,128)(2,1)S(1)}, u32[]{:S(2)}, u32[]{:S(2)}) collective-permute-start(bf16[688,256]{1,0:T(8,128)(2,1)S(1)} %fusion.refs_0_), channel_id=1, source_target_pairs={{0,64},{64,128},{128,192},{192,0},{1,65},{65,129},{129,193},{193,1... | collective-permute-start | bytes 1056776 | tf_op jit(solution)/shard_map/ppermute | solution.py:19
  30.7 11.8 %collective-permute-start.2 = (bf16[688,256]{1,0:T(8,128)(2,1)S(1)}, bf16[688,256]{1,0:T(8,128)(2,1)S(1)}, u32[]{:S(2)}, u32[]{:S(2)}) collective-permute-start(bf16[688,256]{1,0:T(8,128)(2,1)S(1)} %fusion.refs_0_), channel_id=1, source_target_pairs={{0,48},{16,0},{32,16},{48,32},{1,49},{17,1},{33,17},{49,33},{2,50}... | collective-permute-start | bytes 1056776 | tf_op jit(solution)/shard_map/ppermute | solution.py:19
  32.1 17.2 %collective-permute-start.25 = (bf16[688,256]{1,0:T(8,128)(2,1)S(1)}, bf16[688,256]{1,0:T(8,128)(2,1)S(1)}, u32[]{:S(2)}, u32[]{:S(2)}) collective-permute-start(bf16[688,256]{1,0:T(8,128)(2,1)S(1)} %fusion.1.refs_9_), channel_id=1, source_target_pairs={{0,48},{16,0},{32,16},{48,32},{1,49},{17,1},{33,17},{49,33},{2,50}... | collective-permute-start | bytes 1056776 | tf_op jit(solution)/shard_map/ppermute | solution.py:19
  34.9 15.2 %collective-permute-start.22 = (bf16[688,256]{1,0:T(8,128)(2,1)S(1)}, bf16[688,256]{1,0:T(8,128)(2,1)S(1)}, u32[]{:S(2)}, u32[]{:S(2)}) collective-permute-start(bf16[688,256]{1,0:T(8,128)(2,1)S(1)} %fusion.1.refs_9_), channel_id=1, source_target_pairs={{0,16},{16,32},{32,48},{48,0},{1,17},{17,33},{33,49},{49,1},{2,18}... | collective-permute-start | bytes 1056776 | tf_op jit(solution)/shard_map/ppermute | solution.py:19
  35.1 37.1 %collective-permute-start.26 = (bf16[1376,256]{1,0:T(8,128)(2,1)S(1)}, bf16[1376,256]{1,0:T(8,128)(2,1)S(1)}, u32[]{:S(2)}, u32[]{:S(2)}) collective-permute-start(bf16[1376,256]{1,0:T(8,128)(2,1)S(1)} %constant_dynamic-update-slice_fusion.6.refs_10_), channel_id=1, source_target_pairs={{0,48},{16,0},{32,16},{48,32},{1,49},{17,1},{33,17},{49,33},{2,50}... | collective-permute-start | bytes 2113544 | tf_op jit(solution)/shard_map/ppermute | solution.py:19
  41.3 34.7 %collective-permute-start.23 = (bf16[1376,256]{1,0:T(8,128)(2,1)S(1)}, bf16[1376,256]{1,0:T(8,128)(2,1)S(1)}, u32[]{:S(2)}, u32[]{:S(2)}) collective-permute-start(bf16[1376,256]{1,0:T(8,128)(2,1)S(1)} %constant_dynamic-update-slice_fusion.6.refs_10_), channel_id=1, source_target_pairs={{0,16},{16,32},{32,48},{48,0},{1,17},{17,33},{33,49},{49,1},{2,18}... | collective-permute-start | bytes 2113544 | tf_op jit(solution)/shard_map/ppermute | solution.py:19
  42.5 20.2 %collective-permute-start.1 = (bf16[344,256]{1,0:T(8,128)(2,1)S(1)}, bf16[344,256]{1,0:T(8,128)(2,1)S(1)}, u32[]{:S(2)}, u32[]{:S(2)}) collective-permute-start(bf16[344,256]{1,0:T(8,128)(2,1)S(1)} %slice.83), channel_id=1, source_target_pairs={{0,16},{16,32},{32,48},{48,0},{1,17},{17,33},{33,49},{49,1},{2,18}... | collective-permute-start | bytes 528392 | tf_op jit(solution)/shard_map/ppermute | solution.py:19
  49.3 14.9 %collective-permute-start.9 = (bf16[344,256]{1,0:T(8,128)(2,1)S(1)}, bf16[344,256]{1,0:T(8,128)(2,1)S(1)}, u32[]{:S(2)}, u32[]{:S(2)}) collective-permute-start(bf16[344,256]{1,0:T(8,128)(2,1)S(1)} %slice.88), channel_id=1, source_target_pairs={{0,64},{64,128},{128,192},{192,0},{1,65},{65,129},{129,193},{193,1... | collective-permute-start | bytes 528392 | tf_op jit(solution)/shard_map/ppermute | solution.py:19
  50.1 41.7 %collective-permute-start.30 = (bf16[32,128]{1,0:T(8,128)(2,1)S(1)}, bf16[32,128]{1,0:T(8,128)(2,1)S(1)}, u32[]{:S(2)}, u32[]{:S(2)}) collective-permute-start(bf16[32,128]{1,0:T(8,128)(2,1)S(1)} %add.25), channel_id=1, source_target_pairs={{0,4},{1,5},{2,6},{3,7},{4,8},{5,9},{6,10},{7,11},{8,12},{9,13},{1... | collective-permute-start | bytes 24584 | tf_op jit(solution)/shard_map/ppermute | solution.py:19
  68.2 19.1 %collective-permute-start.20 = (bf16[1376,256]{1,0:T(8,128)(2,1)S(1)}, bf16[1376,256]{1,0:T(8,128)(2,1)S(1)}, u32[]{:S(2)}, u32[]{:S(2)}) collective-permute-start(bf16[1376,256]{1,0:T(8,128)(2,1)S(1)} %constant_dynamic-update-slice_fusion.4.refs_1_), channel_id=1, source_target_pairs={{0,192},{64,0},{128,64},{192,128},{1,193},{65,1},{129,65},{193,129... | collective-permute-start | bytes 2113544 | tf_op jit(solution)/shard_map/ppermute | solution.py:19
  72.2 18.0 %collective-permute-start.17 = (bf16[1376,256]{1,0:T(8,128)(2,1)S(1)}, bf16[1376,256]{1,0:T(8,128)(2,1)S(1)}, u32[]{:S(2)}, u32[]{:S(2)}) collective-permute-start(bf16[1376,256]{1,0:T(8,128)(2,1)S(1)} %constant_dynamic-update-slice_fusion.4.refs_1_), channel_id=1, source_target_pairs={{0,64},{64,128},{128,192},{192,0},{1,65},{65,129},{129,193},{193,1... | collective-permute-start | bytes 2113544 | tf_op jit(solution)/shard_map/ppermute | solution.py:19
  72.2 20.3 %collective-permute-start.6 = (bf16[688,256]{1,0:T(8,128)(2,1)S(1)}, bf16[688,256]{1,0:T(8,128)(2,1)S(1)}, u32[]{:S(2)}, u32[]{:S(2)}) collective-permute-start(bf16[688,256]{1,0:T(8,128)(2,1)S(1)} %constant_dynamic-update-slice_fusion.refs_2_), channel_id=1, source_target_pairs={{0,192},{64,0},{128,64},{192,128},{1,193},{65,1},{129,65},{193,129... | collective-permute-start | bytes 1056776 | tf_op jit(solution)/shard_map/ppermute | solution.py:19
  76.0 18.4 %collective-permute-start.4 = (bf16[688,256]{1,0:T(8,128)(2,1)S(1)}, bf16[688,256]{1,0:T(8,128)(2,1)S(1)}, u32[]{:S(2)}, u32[]{:S(2)}) collective-permute-start(bf16[688,256]{1,0:T(8,128)(2,1)S(1)} %constant_dynamic-update-slice_fusion.refs_2_), channel_id=1, source_target_pairs={{0,64},{64,128},{128,192},{192,0},{1,65},{65,129},{129,193},{193,1... | collective-permute-start | bytes 1056776 | tf_op jit(solution)/shard_map/ppermute | solution.py:19
  87.3 11.1 %collective-permute-start.14 = (bf16[688,256]{1,0:T(8,128)(2,1)S(1)}, bf16[688,256]{1,0:T(8,128)(2,1)S(1)}, u32[]{:S(2)}, u32[]{:S(2)}) collective-permute-start(bf16[688,256]{1,0:T(8,128)(2,1)S(1)} %constant_dynamic-update-slice_fusion.2.refs_11_), channel_id=1, source_target_pairs={{0,48},{16,0},{32,16},{48,32},{1,49},{17,1},{33,17},{49,33},{2,50}... | collective-permute-start | bytes 1056776 | tf_op jit(solution)/shard_map/ppermute | solution.py:19
  90.1 11.1 %collective-permute-start.12 = (bf16[688,256]{1,0:T(8,128)(2,1)S(1)}, bf16[688,256]{1,0:T(8,128)(2,1)S(1)}, u32[]{:S(2)}, u32[]{:S(2)}) collective-permute-start(bf16[688,256]{1,0:T(8,128)(2,1)S(1)} %constant_dynamic-update-slice_fusion.2.refs_11_), channel_id=1, source_target_pairs={{0,16},{16,32},{32,48},{48,0},{1,17},{17,33},{33,49},{49,1},{2,18}... | collective-permute-start | bytes 1056776 | tf_op jit(solution)/shard_map/ppermute | solution.py:19
  91.7 19.7 %collective-permute-start.27 = (bf16[1032,256]{1,0:T(8,128)(2,1)S(1)}, bf16[1032,256]{1,0:T(8,128)(2,1)S(1)}, u32[]{:S(2)}, u32[]{:S(2)}) collective-permute-start(bf16[1032,256]{1,0:T(8,128)(2,1)S(1)} %pad_maximum_fusion.3), channel_id=1, source_target_pairs={{0,48},{16,0},{32,16},{48,32},{1,49},{17,1},{33,17},{49,33},{2,50}... | collective-permute-start | bytes 1585160 | tf_op jit(solution)/shard_map/ppermute | solution.py:19
  92.5 19.0 %collective-permute-start.24 = (bf16[1032,256]{1,0:T(8,128)(2,1)S(1)}, bf16[1032,256]{1,0:T(8,128)(2,1)S(1)}, u32[]{:S(2)}, u32[]{:S(2)}) collective-permute-start(bf16[1032,256]{1,0:T(8,128)(2,1)S(1)} %pad_maximum_fusion.2), channel_id=1, source_target_pairs={{0,16},{16,32},{32,48},{48,0},{1,17},{17,33},{33,49},{49,1},{2,18}... | collective-permute-start | bytes 1585160 | tf_op jit(solution)/shard_map/ppermute | solution.py:19
  94.4 20.4 %collective-permute-start.21 = (bf16[1032,256]{1,0:T(8,128)(2,1)S(1)}, bf16[1032,256]{1,0:T(8,128)(2,1)S(1)}, u32[]{:S(2)}, u32[]{:S(2)}) collective-permute-start(bf16[1032,256]{1,0:T(8,128)(2,1)S(1)} %pad_maximum_fusion.1), channel_id=1, source_target_pairs={{0,192},{64,0},{128,64},{192,128},{1,193},{65,1},{129,65},{193,129... | collective-permute-start | bytes 1585160 | tf_op jit(solution)/shard_map/ppermute | solution.py:19
  98.4 20.5 %collective-permute-start.18 = (bf16[1032,256]{1,0:T(8,128)(2,1)S(1)}, bf16[1032,256]{1,0:T(8,128)(2,1)S(1)}, u32[]{:S(2)}, u32[]{:S(2)}) collective-permute-start(bf16[1032,256]{1,0:T(8,128)(2,1)S(1)} %pad_maximum_fusion), channel_id=1, source_target_pairs={{0,64},{64,128},{128,192},{192,0},{1,65},{65,129},{129,193},{193,1... | collective-permute-start | bytes 1585160 | tf_op jit(solution)/shard_map/ppermute | solution.py:19
  108.8 11.6 %collective-permute-start.7 = (bf16[344,256]{1,0:T(8,128)(2,1)S(1)}, bf16[344,256]{1,0:T(8,128)(2,1)S(1)}, u32[]{:S(2)}, u32[]{:S(2)}) collective-permute-start(bf16[344,256]{1,0:T(8,128)(2,1)S(1)} %slice.86), channel_id=1, source_target_pairs={{0,192},{64,0},{128,64},{192,128},{1,193},{65,1},{129,65},{193,129... | collective-permute-start | bytes 528392 | tf_op jit(solution)/shard_map/ppermute | solution.py:19
  (26 other events, 276.7 us)
